TPU v7x, 32 devices: a whole 2x2x4 slice. The times are simulated.
32 devices in a mesh: row: 4 (over z), col: 8 (over y, x, core).
Axes of the slice: x: 2, y: 2, z: 4, core: 2. Of those that a mesh axis runs over, the one named last changes fastest.
Arguments:
- neighbor: int32 [32, 3072, 3072], P(None, 'col', 'row'), may hold values from 0 to 1, as said below
- true_coords: float32 [32, 3, 3072], P(None, None, ('row', 'col')), as said below
- pred_coords: float32 [32, 3, 3072], P(None, None, ('row', 'col')), as said below
- residue_mask: int32 [32, 3072], P(None, ('row', 'col')), may hold values from 0 to 1, as said below
- single: bfloat16 [32, 3072, 384], P(None, ('row', 'col'))
- ln_gain: float32 [384], replicated, may hold values from 0.1 to 1.9
- w_hidden: bfloat16 [384, 128], replicated, may hold values from -0.3125 to 0.3125
- b_hidden: float32 [128], replicated, may hold values from -3 to 3
- w_mid: bfloat16 [128, 128], replicated, may hold values from -0.5 to 0.5
- b_mid: float32 [128], replicated, may hold values from -3 to 3
- w_logits: bfloat16 [128, 50], replicated, may hold values from -1.5 to 1.5
- b_logits: float32 [50], replicated, may hold values from -4 to 4
Outputs:
- lddt_score: float32 [32, 3072], P(None, ('row', 'col'))
- residue_loss: float32 [32, 3072], P(None, ('row', 'col'))
- total_loss: float32 [], replicated
Inputs may be any that keep to these rules, and one draw needn't show every extreme that they name: `neighbor`: 0 or 1; 0 where j == i; 1 wherever 0 < |i - j| <= 8. `residue_mask`: per structure, 1 on a leading run of 1536 or more residues and 0 after it. `true_coords`: positions in angstroms. `pred_coords`: positions in angstroms.
All inputs are finite; a program needn't handle non-finite values.
Results may differ from a plain program's by a relative error of at most 0.00098.
Values sent between devices are 32-bit elements; how exact they have to be, the bound alone decides.
A program may use at most 128 MiB of HBM per device.

v0:
```python
import jax
import jax.numpy as jnp
from jax import lax
from jax.sharding import PartitionSpec as P

L = 3072
THRESHOLDS = (0.5, 1.0, 2.0, 4.0)


def from_root(shard, axis, root):
    mine = lax.axis_index(axis) == root
    return lax.psum(jnp.where(mine, shard, jnp.zeros_like(shard)), axis)


def tile_dist(rows_block, cols_block):
    total = (cols_block[:, 0, :, None] - rows_block[:, 0, None, :]) ** 2
    total = total + (cols_block[:, 1, :, None] - rows_block[:, 1, None, :]) ** 2
    total = total + (cols_block[:, 2, :, None] - rows_block[:, 2, None, :]) ** 2
    return jnp.sqrt(total + 1e-10)


def head_loss(lddt_value, single, ln_gain, w_hidden, b_hidden, w_mid, b_mid, w_logits, b_logits):
    features = single.astype(jnp.float32)
    average = jnp.mean(features, axis=-1, keepdims=True)
    centred = features - average
    variance = jnp.mean(centred * centred, axis=-1, keepdims=True)
    normed = (centred * lax.rsqrt(variance + 1e-05) * ln_gain).astype(jnp.bfloat16)
    first_hidden = jax.nn.relu(
        jnp.dot(normed, w_hidden, preferred_element_type=jnp.float32) + b_hidden
    ).astype(jnp.bfloat16)
    second_hidden = jax.nn.relu(
        jnp.dot(first_hidden, w_mid, preferred_element_type=jnp.float32) + b_mid
    ).astype(jnp.bfloat16)
    logits = jnp.dot(second_hidden, w_logits, preferred_element_type=jnp.float32) + b_logits
    log_total = jnp.log(jnp.sum(jnp.exp(logits), axis=-1))
    bins = logits.shape[-1]
    centers = (jnp.arange(bins).astype(jnp.float32) + 0.5) / bins
    closeness = jnp.exp(-((lddt_value[..., None] - centers) ** 2) * (bins * bins * 0.5))
    target = closeness / jnp.sum(closeness, axis=-1, keepdims=True)
    return log_total - jnp.sum(target * logits, axis=-1)


def local(
    neighbor,
    true_coords,
    pred_coords,
    residue_mask,
    single,
    ln_gain,
    w_hidden,
    b_hidden,
    w_mid,
    b_mid,
    w_logits,
    b_logits,
):
    valid = residue_mask.astype(jnp.float32)
    own_len = residue_mask.shape[1]
    stacked = jnp.concatenate([true_coords, pred_coords, valid[:, None, :]], axis=1)
    row_count = lax.axis_size("row")
    col_count = lax.axis_size("col")
    rows_len = L // row_count
    cols_len = L // col_count
    col_index = lax.axis_index("col")
    rows_part = lax.all_gather(stacked, "col", axis=2, tiled=True)
    offset = col_index * cols_len % rows_len
    column_piece = lax.dynamic_slice_in_dim(rows_part, offset, cols_len, 2)
    source_row = col_index * cols_len // rows_len
    cols_part = from_root(column_piece, "row", source_row)
    true_dist = tile_dist(rows_part[:, 0:3], cols_part[:, 0:3])
    pred_dist = tile_dist(rows_part[:, 3:6], cols_part[:, 3:6])
    mismatch = jnp.abs(pred_dist - true_dist)
    scores = jnp.zeros_like(mismatch)
    for threshold in THRESHOLDS:
        scores = scores + jax.nn.sigmoid(4.0 * (threshold - mismatch))
    scores = 0.25 * scores
    weights = neighbor.astype(jnp.float32) * rows_part[:, 6, None, :] * cols_part[:, 6, :, None]
    preserved = jnp.sum(weights * scores, axis=1)
    neighbors = jnp.sum(weights, axis=1)
    preserved_all, neighbors_all = lax.psum((preserved, neighbors), "col")
    preserved_own = lax.dynamic_slice_in_dim(preserved_all, col_index * own_len, own_len, 1)
    neighbors_own = lax.dynamic_slice_in_dim(neighbors_all, col_index * own_len, own_len, 1)
    lddt_score = preserved_own / jnp.maximum(neighbors_own, 1.0)
    residue_loss = valid * head_loss(
        lddt_score, single, ln_gain, w_hidden, b_hidden, w_mid, b_mid, w_logits, b_logits
    )
    loss_sum, valid_sum = lax.psum((jnp.sum(residue_loss), jnp.sum(valid)), ("row", "col"))
    total_loss = loss_sum / valid_sum
    return (lddt_score, residue_loss, total_loss)


def solution(mesh):
    placed = (
        P(None, "col", "row"),
        P(None, None, ("row", "col")),
        P(None, None, ("row", "col")),
        P(None, ("row", "col")),
        P(None, ("row", "col"), None),
        P(),
        P(),
        P(),
        P(),
        P(),
        P(),
        P(),
    )
    return jax.shard_map(
        local,
        mesh=mesh,
        in_specs=placed,
        out_specs=(P(None, ("row", "col")), P(None, ("row", "col")), P()),
        check_vma=False,
    )
```

profile of v0, /device:TPU:0, one launch (start us, length us, event | category | flops | bytes accessed | tf_op | source)
XLA Modules:
  0.0 312.7 jit_solution(15335422747212448188)
XLA Ops:
  7.3 0.7 convert_bitcast_fusion
  8.0 0.8 pad_maximum_fusion
  8.8 0.9 copy.33
  9.7 21.3 %all_gather.3 = f32[32,7,768]{0,1,2:T(8,128)S(1)} all-gather(f32[32,7,96]{0,1,2:T(8,128)} %copy.33), channel_id=1, replica_groups=mesh['row'=4,'col'=8] {'col'}, dimensions={2}, use_global_device_ids=true | all-gather | bytes 774144 | tf_op jit(solution)/shard_map/all_gather | solution.py:65
  31.0 1.3 dynamic-slice_select_fusion
  32.4 3.3 %fusion.31 = (f32[32,1,768]{0,1,2:T(1,128)}, f32[32,1,768]{0,1,2:T(1,128)}, f32[32,1,768]{0,1,2:T(1,128)}, f32[32,1,768]{0,1,2:T(1,128)}, f32[32,1,768]{0,1,2:T(...) fusion(f32[32,7,768]{0,1,2:T(8,128)S(1)} %all_gather.3), kind=kLoop, calls=%fused_computation.43 | loop fusion | bytes 1376256 | tf_op jit(solution)/shard_map/slice | solution.py:77
  35.6 2.3 convert_reduce_fusion
  37.9 2.8 fusion.4
  40.8 3.2 %maximum_convert_fusion = bf16[32,96,128]{2,1,0:T(8,128)(2,1)S(1)} fusion(bf16[32,96,384]{2,1,0:T(8,128)(2,1)} %param.16, f32[384]{0:T(512)} %param.17, f32[32,96]{1,0:T(8,128)S(1)} %add_rsqrt_fusion, f32[32,96]{1,0:T(8,128)S(1)} %broadcast_multiply_fusion, f32[128]{0:T(128)} %param.21, f32[128]{0:T(128)} %param.19, bf16[384,128]{1,0:T(8,128)(2,1)S(1)} %copy-done, ...), kind=kOutput, calls=%fused_computation.15 | convolution fusion | flops 410910720 | bytes 3303936 | tf_op jit(solution)/shard_map/dot_general | solution.py:32
  44.0 1.1 copy.34
  45.1 1.1 copy.37
  46.2 1.1 copy.39
  47.4 1.1 copy.41
  48.5 1.1 copy.43
  49.7 1.1 copy.45
  50.8 1.1 copy.47
  51.9 1.4 exponential_reduce_fusion
  53.4 48.4 %all-reduce.5.cloned.1.call-done = f32[32,7,384]{0,1,2:T(8,128)} async-done(((f32[32,7,384]{0,1,2:T(8,128)}), f32[32,7,384]{0,1,2:T(8,128)}) %all-reduce.5.cloned.1.call-update) | async-done | bytes 344080 | tf_op jit(solution)/shard_map/psum | solution.py:12
  101.7 6.8 %fusion.32 = (f32[32,1,384]{0,1,2:T(1,128)S(1)}, f32[32,1,384]{0,1,2:T(1,128)S(1)}, f32[32,1,384]{0,1,2:T(1,128)S(1)}, f32[32,1,384]{0,1,2:T(1,128)S(1)}, f32[32...) fusion(f32[32,7,384]{0,1,2:T(8,128)} %all-reduce.5.cloned.1.call-done), kind=kLoop, calls=%fused_computation.44 | loop fusion | bytes 688128 | tf_op jit(solution)/shard_map/slice | solution.py:77
  108.5 0.1 copy.35
  108.6 0.1 copy.36
  108.7 0.1 copy.38
  108.8 0.1 copy.40
  108.9 0.1 copy.42
  109.1 0.1 copy.44
  109.2 0.1 copy.46
  109.3 98.8 %multiply_reduce_fusion = (f32[32,768]{1,0:T(8,128)}, f32[32,768]{1,0:T(8,128)}) fusion(s32[32,384,768]{2,1,0:T(8,128)} %param.12, f32[32,768]{1,0:T(8,128)S(1)} %copy.47, f32[32,384]{1,0:T(8,128)S(1)} %copy.46, f32[32,768]{1,0:T(8,128)S(1)} %copy.45, f32[32,384]{1,0:T(8,128)S(1)} %copy.44, f32[32,768]{1,0:T(8,128)S(1)} %copy.43, f32[32,384]{1,0:T(8,128)S(1)} %copy.42, ...), kind=kLoop, calls=%fused_computation.1 | loop fusion | flops 471810048 | bytes 38977536 | tf_op jit(solution)/shard_map/reduce_sum | solution.py:78
  208.2 53.1 %all-reduce.7.cloned.1.call-done = (f32[32,768]{1,0:T(8,128)}, f32[32,768]{1,0:T(8,128)}) async-done(((f32[32,768]{1,0:T(8,128)}, f32[32,768]{1,0:T(8,128)}), (f32[32,768]{1,0:T(8,128)}, f32[32,768]{1,0:T(8,128)})) %all-reduce.7.cloned.1.call-update) | async-done | bytes 196624 | tf_op jit(solution)/shard_map/psum | solution.py:80
  261.3 0.9 maximum_divide_fusion
  262.1 0.4 fusion.33
  262.6 1.3 fusion.30
  263.9 39.6 %all-reduce = (f32[]{:T(128)}, f32[]{:T(128)}) all-reduce(f32[]{:T(128)} %get-tuple-element.12, f32[]{:T(128)} %get-tuple-element.28), channel_id=1, replica_groups=mesh['row'=4,'col'=8] {'row','col'}, use_global_device_ids=true, to_apply=%region_11.12 | all-reduce | flops 2 | bytes 16 | tf_op jit(solution)/shard_map/psum | solution.py:87
  (13 shorter events, 0.2 us)
Async XLA Ops:
  7.2 33.6 %copy-start = (bf16[384,128]{1,0:T(8,128)(2,1)S(1)}, bf16[384,128]{1,0:T(8,128)(2,1)}, u32[]{:S(2)}) copy-start(bf16[384,128]{1,0:T(8,128)(2,1)} %param.18) | copy-start | bytes 294916
  7.2 94.6 %all-reduce.5.cloned.1.call-start = ((), (), s32[]{:S(2)}) async-start(), calls=%async_computation | async-start | bytes 3145728 | tf_op jit(solution)/shard_map/psum | solution.py:12
  32.3 228.9 %all-reduce.7.cloned.1.call-start = ((), (), s32[]{:S(2)}) async-start(), calls=%async_computation.1 | async-start | bytes 393216 | tf_op jit(solution)/shard_map/psum | solution.py:80
  109.3 153.3 %copy-start.1 = (s32[32,96]{1,0:T(8,128)S(1)}, s32[32,96]{1,0:T(8,128)}, u32[]{:S(2)}) copy-start(s32[32,96]{1,0:T(8,128)} %param.15) | copy-start | bytes 36868
  262.1 42.6 %copy-start.2 = (f32[32,96]{1,0:T(8,128)}, f32[32,96]{1,0:T(8,128)S(1)}, u32[]{:S(2)}) copy-start(f32[32,96]{1,0:T(8,128)S(1)} %maximum_divide_fusion) | copy-start | bytes 36868
Sparse Core Ops, SparseCore 0:
  32.5 69.2 all-reduce.4
  208.3 52.9 all-reduce.6
where the time goes:
time: 314 us; the launch traced here: 313 us
  other arithmetic  109 us (35%)
  waiting for transfers between devices  102 us (32%)
  blocking collectives  60.8 us (19%)
  local copies, waits for them, and re-layouts  19.7 us (6%)
  between operations  16.6 us (5%)
  matrix products  4.59 us (1%)
    reduce_sum x1, other arithmetic, local(): preserved = jnp.sum(weights * scores, axis=1)  98.8 us
    psum x1, waiting for transfers between devices, local(): preserved_all, neighbors_all = lax.psum((preserved, neighbors), 'col')  53.1 us
    psum x1, waiting for transfers between devices, from_root(): return lax.psum(jnp.where(mine, shard, jnp.zeros_like(shard)), axis)  48.4 us
    psum x1, blocking collectives, local(): lax.psum((jnp.sum(residue_loss), jnp.sum(valid)), ('row', 'col'))  39.6 us
    all_gather x1, blocking collectives, local(): rows_part = lax.all_gather(stacked, 'col', axis=2, tiled=True)  21.3 us
    slice x1, local copies, waits for them, and re-layouts, local(): cols_part[:, 6, :, None]  6.78 us
  transfers between devices with their start and end apart: 2, of which 2 were waited for; matrix products, arithmetic and copies ran while one was open for 7% of the time, Pallas kernels for 0%

commit v1 on v0

--- a/solution.py
+++ b/solution.py
@@ -62,7 +62,9 @@
     rows_len = L // row_count
     cols_len = L // col_count
     col_index = lax.axis_index("col")
-    rows_part = lax.all_gather(stacked, "col", axis=2, tiled=True)
+    rows_part = jnp.concatenate(
+        lax.all_to_all(jnp.stack([stacked] * lax.axis_size("col")), "col", 0, 0), axis=2
+    )
     offset = col_index * cols_len % rows_len
     column_piece = lax.dynamic_slice_in_dim(rows_part, offset, cols_len, 2)
     source_row = col_index * cols_len // rows_len

time: 314 us -> 273 us (0.87)
  blocking collectives: 60.8 us -> 39.6 us
  local copies, waits for them, and re-layouts: 19.7 us -> 2.91 us
  waiting for transfers between devices: 102 us -> 94 us
  starting transfers between devices: 0.08 us -> 5.28 us
    all_gather x1 -> x0, blocking collectives: 21.3 us -> none  [local(): rows_part = lax.all_gather(stacked, 'col', axis=2, tiled=True)]
    psum x1, waiting for transfers between devices: 48.4 us -> 34.5 us  [from_root(): return lax.psum(jnp.where(mine, shard, jnp.zeros_like(shard)), axis)]
    slice x2 -> x0, local copies, waits for them, and re-layouts: 10 us -> none  [the longest x1 6.78 us: local(): cols_part[:, 6, :, None]]
    sub x12 -> x0, local copies, waits for them, and re-layouts: 7.5 us -> none  [the longest x4 2.5 us: tile_dist(): total = total + (cols_block[:, 1, :, None] - rows_block[:, 1, None, :]) ** 2]
    all_to_all x0 -> x1, waiting for transfers between devices: none -> 5.61 us  [local(): lax.all_to_all(jnp.stack([stacked] * lax.axis_size('col')), 'col', 0, 0)]
    all_to_all x0 -> x1, starting transfers between devices: none -> 5.2 us  [local(): lax.all_to_all(jnp.stack([stacked] * lax.axis_size('col')), 'col', 0, 0)]
  transfers between devices with their start and end apart: 2 -> 3, of which waited for: 2 -> 3; matrix products, arithmetic and copies ran while one was open for 7% -> 4% of each run, Pallas kernels for 0% -> 0%
where the time goes in v1:
time: 273 us; the launch traced here: 272 us
  other arithmetic  109 us (40%)
  waiting for transfers between devices  94 us (34%)
  blocking collectives  39.6 us (15%)
  between operations  16.6 us (6%)
  starting transfers between devices  5.28 us (2%)
  matrix products  4.58 us (2%)
  local copies, waits for them, and re-layouts  2.91 us (1%)
    reduce_sum x1, other arithmetic, local(): preserved = jnp.sum(weights * scores, axis=1)  98.8 us
    psum x1, waiting for transfers between devices, local(): preserved_all, neighbors_all = lax.psum((preserved, neighbors), 'col')  53.8 us
    psum x1, blocking collectives, local(): lax.psum((jnp.sum(residue_loss), jnp.sum(valid)), ('row', 'col'))  39.6 us
    psum x1, waiting for transfers between devices, from_root(): return lax.psum(jnp.where(mine, shard, jnp.zeros_like(shard)), axis)  34.5 us
    all_to_all x1, waiting for transfers between devices, local(): lax.all_to_all(jnp.stack([stacked] * lax.axis_size('col')), 'col', 0, 0)  5.61 us
  transfers between devices with their start and end apart: 3, of which 3 were waited for; matrix products, arithmetic and copies ran while one was open for 4% of the time, Pallas kernels for 0%

profile of v1, /device:TPU:0, one launch (start us, length us, event | category | flops | bytes accessed | tf_op | source)
XLA Modules:
  0.0 271.9 jit_solution(17500677256714118818)
XLA Ops:
  7.2 0.0 copy-start
  7.2 0.8 convert_bitcast_fusion
  7.9 0.8 pad_maximum_fusion
  8.8 1.0 stack.2
  9.8 5.2 %all-to-all-start = ((f32[8,32,7,96]{3,1,2,0:T(8,128)}), f32[8,32,7,96]{3,1,2,0:T(8,128)S(1)}, u32[]{:S(2)}, u32[]{:S(2)}) async-start(f32[8,32,7,96]{3,1,2,0:T(8,128)} %stack.2), calls=%async_computation | async-start | bytes 1835008 | tf_op jit(solution)/shard_map/all_to_all | solution.py:66
  15.0 0.0 all-reduce.5.cloned.1.call-start
  15.1 2.3 convert_reduce_fusion
  17.4 2.8 %fusion.4 = f32[32,96]{1,0:T(8,128)S(1)} fusion(bf16[32,96,384]{2,1,0:T(8,128)(2,1)} %param.16, f32[32,96]{1,0:T(8,128)S(1)} %broadcast_multiply_fusion), kind=kLoop, calls=%fused_computation.8 | loop fusion | flops 4715520 | bytes 2383872 | tf_op jit(solution)/shard_map/reduce_sum | solution.py:26
  20.2 0.0 copy-done
  20.2 3.2 %maximum_convert_fusion = bf16[32,96,128]{2,1,0:T(8,128)(2,1)S(1)} fusion(bf16[32,96,384]{2,1,0:T(8,128)(2,1)} %param.16, f32[384]{0:T(512)} %param.17, f32[32,96]{1,0:T(8,128)S(1)} %add_rsqrt_fusion, f32[32,96]{1,0:T(8,128)S(1)} %broadcast_multiply_fusion, f32[128]{0:T(128)} %param.21, f32[128]{0:T(128)} %param.19, bf16[384,128]{1,0:T(8,128)(2,1)S(1)} %copy-done, ...), kind=kOutput, calls=%fused_computation.15 | convolution fusion | flops 410910720 | bytes 3303936 | tf_op jit(solution)/shard_map/dot_general | solution.py:32
  23.4 5.6 %all-to-all-done = f32[8,32,7,96]{3,1,2,0:T(8,128)S(1)} async-done(((f32[8,32,7,96]{3,1,2,0:T(8,128)}), f32[8,32,7,96]{3,1,2,0:T(8,128)S(1)}, u32[]{:S(2)}, u32[]{:S(2)}) %all-to-all-start) | async-done | bytes 688160 | tf_op jit(solution)/shard_map/all_to_all | solution.py:66
  29.0 0.5 copy.15
  29.5 0.3 reshape.46
  29.8 0.9 dynamic-slice_select_fusion
  30.7 0.0 all-reduce.5.cloned.1.call-update
  30.8 0.0 all-reduce.7.cloned.1.call-start
  30.8 1.4 exponential_reduce_fusion
  32.3 34.5 %all-reduce.5.cloned.1.call-done = f32[32,7,384]{2,0,1:T(8,128)} async-done(((f32[32,7,384]{2,0,1:T(8,128)}), f32[32,7,384]{2,0,1:T(8,128)}) %all-reduce.5.cloned.1.call-update) | async-done | bytes 344080 | tf_op jit(solution)/shard_map/psum | solution.py:12
  66.8 1.0 slice_bitcast_fusion.13
  67.8 0.0 copy-start.1
  67.8 98.8 %multiply_reduce_fusion = (f32[32,768]{1,0:T(8,128)}, f32[32,768]{1,0:T(8,128)}) fusion(s32[32,384,768]{2,1,0:T(8,128)} %param.12, f32[32,768]{1,0:T(8,128)S(1)} %get-tuple-element.12, f32[32,384]{1,0:T(8,128)S(1)} %get-tuple-element.19, f32[32,768]{1,0:T(8,128)S(1)} %get-tuple-element.13, f32[32,384]{1,0:T(8,128)S(1)} %get-tuple-element.20, ...), kind=kLoop, calls=%fused_computation.1 | loop fusion | flops 471810048 | bytes 38977536 | tf_op jit(solution)/shard_map/reduce_sum | solution.py:80
  166.7 0.0 all-reduce.7.cloned.1.call-update
  166.7 53.8 %all-reduce.7.cloned.1.call-done = (f32[32,768]{1,0:T(8,128)}, f32[32,768]{1,0:T(8,128)}) async-done(((f32[32,768]{1,0:T(8,128)}, f32[32,768]{1,0:T(8,128)}), (f32[32,768]{1,0:T(8,128)}, f32[32,768]{1,0:T(8,128)})) %all-reduce.7.cloned.1.call-update) | async-done | bytes 196624 | tf_op jit(solution)/shard_map/psum | solution.py:82
  220.5 0.9 maximum_divide_fusion
  221.3 0.0 copy-start.2
  221.4 0.4 fusion.31
  221.8 0.0 copy-done.1
  221.8 1.3 fusion.30
  223.1 39.6 %all-reduce = (f32[]{:T(128)}, f32[]{:T(128)}) all-reduce(f32[]{:T(128)} %get-tuple-element.9, f32[]{:T(128)} %get-tuple-element.25), channel_id=1, replica_groups=mesh['row'=4,'col'=8] {'row','col'}, use_global_device_ids=true, to_apply=%region_11.12 | all-reduce | flops 2 | bytes 16 | tf_op jit(solution)/shard_map/psum | solution.py:89
  263.9 0.0 copy-done.2
  (4 shorter events, 0.1 us)
Async XLA Ops:
  7.2 13.0 %copy-start = (bf16[384,128]{1,0:T(8,128)(2,1)S(1)}, bf16[384,128]{1,0:T(8,128)(2,1)}, u32[]{:S(2)}) copy-start(bf16[384,128]{1,0:T(8,128)(2,1)} %param.18) | copy-start | bytes 294916
  9.8 19.2 %all-to-all-start = ((f32[8,32,7,96]{3,1,2,0:T(8,128)}), f32[8,32,7,96]{3,1,2,0:T(8,128)S(1)}, u32[]{:S(2)}, u32[]{:S(2)}) async-start(f32[8,32,7,96]{3,1,2,0:T(8,128)} %stack.2), calls=%async_computation | async-start | bytes 1835008 | tf_op jit(solution)/shard_map/all_to_all | solution.py:66
  15.0 51.8 %all-reduce.5.cloned.1.call-start = ((), (), s32[]{:S(2)}) async-start(), calls=%async_computation.1 | async-start | bytes 688128 | tf_op jit(solution)/shard_map/psum | solution.py:12
  30.8 189.7 %all-reduce.7.cloned.1.call-start = ((), (), s32[]{:S(2)}) async-start(), calls=%async_computation.2 | async-start | bytes 393216 | tf_op jit(solution)/shard_map/psum | solution.py:82
  67.8 154.0 %copy-start.1 = (s32[32,96]{1,0:T(8,128)S(1)}, s32[32,96]{1,0:T(8,128)}, u32[]{:S(2)}) copy-start(s32[32,96]{1,0:T(8,128)} %param.15) | copy-start | bytes 36868
  221.3 42.6 %copy-start.2 = (f32[32,96]{1,0:T(8,128)}, f32[32,96]{1,0:T(8,128)S(1)}, u32[]{:S(2)}) copy-start(f32[32,96]{1,0:T(8,128)S(1)} %maximum_divide_fusion) | copy-start | bytes 36868
Sparse Core Ops, SparseCore 0:
  30.9 35.9 all-reduce.4
  166.8 53.6 all-reduce.6
